TPU v7x, 32 devices: a whole 2x2x4 slice. The times are simulated.
32 devices in a mesh: wide: 16 (over z, y, core), narrow: 2 (over x).
Axes of the slice: x: 2, y: 2, z: 4, core: 2. Of those that a mesh axis runs over, the one named last changes fastest.
Arguments:
- query_coords: float32 [3, 32, 16, 32], P(None, ('wide', 'narrow')), may hold values from -1 to 1
- owner_element: int32 [32, 16, 32], P(('wide', 'narrow')), may hold values from 0 to 15
- pair_counts: int32 [32, 32], P(('wide', 'narrow')), may hold values from 0 to 16, as said below
- fields: bfloat16 [512, 8, 1024], P(('wide', 'narrow')), may hold values from -6 to 6
Outputs:
- values: bfloat16 [16, 32, 16, 32], P(None, ('wide', 'narrow'))
Inputs may be any that keep to these rules, and one draw needn't show every extreme that they name: `pair_counts`: every count is at most 16, and some pair of devices reaches 16 in every draw.
All inputs are finite; a program needn't handle non-finite values.
Results may differ from a plain program's by a relative error of at most 0.0043.
Values may be sent and summed in bfloat16 or wider, within the bound.
No kernel may reach another device: no remote copies, remote signals or barrier semaphores. Data moves between devices by JAX's collectives and lax.ppermute only.
A program may use at most 64 MiB of HBM per device.

v0:
```python
import math
import jax
import jax.numpy as jnp
from jax import lax
from jax.sharding import PartitionSpec as P

GLL_NODES = (
    -1.0,
    -0.8717401485096066,
    -0.5917001814331423,
    -0.2092992179024789,
    0.2092992179024789,
    0.5917001814331423,
    0.8717401485096066,
    1.0,
)


def for_sending(shard):
    return jax.tree.map(lambda a: a.astype(jnp.bfloat16) if a.dtype == jnp.float32 else a, shard)


def lagrange(position):
    result = []
    for i in range(8):
        factor = jnp.ones_like(position)
        for m in range(8):
            if m != i:
                factor = factor * ((position - GLL_NODES[m]) / (GLL_NODES[i] - GLL_NODES[m]))
        result.append(factor)
    return jnp.stack(result)


def interpolate(payload, field_table):
    element_count = field_table.shape[0] // 8
    column_count = field_table.shape[1]
    half_cols = column_count // 2
    basis_r = lagrange(payload[0]).astype(jnp.bfloat16)
    tensor_st = (lagrange(payload[1])[:, None, :] * lagrange(payload[2])[None, :, :]).reshape(
        64, -1
    )
    picked = payload[3][None, :] == jnp.arange(element_count, dtype=jnp.float32)[:, None]
    weights = jnp.where(
        picked[:, None, :], basis_r[None, :, :], jnp.zeros((), jnp.bfloat16)
    ).reshape(element_count * 8, -1)
    halves = []
    for h in range(2):
        partial_value = lax.dot_general(
            field_table[:, h * half_cols : (h + 1) * half_cols],
            weights,
            (((0,), (0,)), ((), ())),
            preferred_element_type=jnp.float32,
        )
        halves.append(
            jnp.sum(partial_value.reshape(half_cols // 64, 64, -1) * tensor_st[None, :, :], axis=1)
        )
    return jnp.concatenate(halves, axis=0).astype(jnp.bfloat16)


def evaluate(payload, field_table):
    field_count = field_table.shape[1] // 64
    lead_shape = payload.shape[1:]
    flat = payload.reshape(4, -1)
    total_rows = flat.shape[1]
    block_rows = math.gcd(total_rows, 512)
    blocks = jnp.transpose(flat.reshape(4, total_rows // block_rows, block_rows), (1, 0, 2))

    def one_block(block):
        return interpolate(block, field_table)

    results = lax.map(one_block, blocks)
    return jnp.transpose(results, (1, 0, 2)).reshape((field_count,) + lead_shape)


def on_device(query_coords, owner_element, pair_counts, fields):
    wide_size = lax.axis_size("wide")
    narrow_size = lax.axis_size("narrow")
    device_count = wide_size * narrow_size
    slot_count = owner_element.shape[1]
    element_count = fields.shape[0]
    field_table = fields.reshape(element_count * fields.shape[1], fields.shape[2])
    live = jnp.arange(slot_count, dtype=jnp.int32)[:, None] < pair_counts[0][None, :]
    element_float = jnp.where(live, owner_element[0], element_count).astype(jnp.float32)
    payload = jnp.concatenate([query_coords[:, 0], element_float[None]], axis=0)
    payload = payload.reshape(4, slot_count, wide_size, narrow_size)
    arrived = lax.all_to_all(
        lax.all_to_all(payload, "wide", split_axis=2, concat_axis=2, tiled=True),
        "narrow",
        split_axis=3,
        concat_axis=3,
        tiled=True,
    )
    result = evaluate(arrived, field_table)
    returned = lax.all_to_all(
        lax.all_to_all(for_sending(result), "wide", split_axis=2, concat_axis=2, tiled=True),
        "narrow",
        split_axis=3,
        concat_axis=3,
        tiled=True,
    ).astype(result.dtype)
    return returned.reshape(returned.shape[0], 1, slot_count, device_count)


def solution(mesh):
    placed = (
        P(None, ("wide", "narrow"), None, None),
        P(("wide", "narrow"), None, None),
        P(("wide", "narrow"), None),
        P(("wide", "narrow"), None, None),
    )
    return jax.shard_map(
        on_device,
        mesh=mesh,
        in_specs=placed,
        out_specs=P(None, ("wide", "narrow"), None, None),
        check_vma=False,
    )
```

profile of v0, /device:TPU:0, one launch (start us, length us, event | category | flops | bytes accessed | tf_op | source)
XLA Modules:
  0.0 51.5 jit_solution(9558058476863743550)
XLA Ops:
  0.0 0.8 %copy.35 = s32[1,16,32]{1,2,0:T(8,128)S(1)} copy(s32[1,16,32]{2,1,0:T(8,128)} %param.5) | data formatting | bytes 4096 | tf_op args[1]
  0.9 0.7 %copy-done.2 = s32[1,32]{1,0:T(1,128)S(1)} copy-done((s32[1,32]{1,0:T(1,128)S(1)}, s32[1,32]{1,0:T(1,128)}, u32[]{:S(2)}) %copy-start.2) | copy-done | bytes 152
  1.8 13.7 %all_to_all.20 = f32[16,1,128]{2,1,0:T(1,128)S(1)} all-to-all(f32[16,1,128]{2,1,0:T(1,128)S(1)} %reshape.2410), channel_id=1, replica_groups=mesh['wide'=16,'narrow'=2] {'wide'}, dimensions={0} | all-to-all | bytes 16384 | tf_op jit(solution)/shard_map/all_to_all | solution.py:87
  15.4 0.5 broadcast.3145
  15.9 0.7 %reduce = f32[16,128]{1,0:T(8,128)S(1)} reduce(f32[16,1,128]{2,1,0:T(1,128)S(1)} %all_to_all.20, f32[]{:T(128)} %broadcast.3145), dimensions={1}, to_apply=%all_to_all.12.reduce_sub_computation | reduce | bytes 16388 | tf_op jit(solution)/shard_map/all_to_all | solution.py:87
  16.9 6.4 %all_to_all.21 = f32[2,1,1024]{2,1,0:T(1,128)S(1)} all-to-all(f32[2,1,1024]{2,1,0:T(1,128)S(1)} %reshape.2412), channel_id=1, replica_groups=mesh['wide'=16,'narrow'=2] {'narrow'}, dimensions={0} | all-to-all | bytes 16384 | tf_op jit(solution)/shard_map/all_to_all | solution.py:86
  23.2 0.7 %reduce.1 = f32[2,1024]{1,0:T(2,128)S(1)} reduce(f32[2,1,1024]{2,1,0:T(1,128)S(1)} %all_to_all.21, f32[]{:T(128)} %broadcast.3145), dimensions={1}, to_apply=%all_to_all.13.reduce_sub_computation | reduce | bytes 16388 | tf_op jit(solution)/shard_map/all_to_all | solution.py:86
  24.2 0.2 copy.38
  24.6 0.2 copy.57
  25.2 0.2 copy.56
  25.5 0.2 copy.62
  25.9 0.2 copy.54
  26.2 0.2 copy.46
  26.5 0.2 copy.45
  26.9 0.2 copy.44
  27.2 0.2 copy.43
  27.6 0.2 copy.42
  27.9 0.2 copy.41
  28.3 0.2 copy.39
  28.7 0.2 copy.40
  29.0 0.2 copy.53
  29.3 0.2 copy.52
  29.7 0.2 copy.51
  30.0 0.2 copy.50
  32.7 0.5 copy-done
  33.2 0.3 fusion
  33.5 0.4 multiply_reduce_fusion.1
  34.2 0.4 copy_bitcast_fusion.1
  34.8 9.1 %all_to_all.22 = bf16[16,2,256]{2,1,0:T(2,128)(2,1)S(1)} all-to-all(bf16[16,2,256]{2,1,0:T(2,128)(2,1)S(1)} %reshape.2414), channel_id=1, replica_groups=mesh['wide'=16,'narrow'=2] {'wide'}, dimensions={0} | all-to-all | bytes 32768 | tf_op jit(solution)/shard_map/all_to_all | solution.py:95
  44.2 6.2 %all_to_all.23 = bf16[2,2,2048]{2,1,0:T(2,128)(2,1)S(1)} all-to-all(bf16[2,2,2048]{2,1,0:T(2,128)(2,1)S(1)} %reshape.2416), channel_id=1, replica_groups=mesh['wide'=16,'narrow'=2] {'narrow'}, dimensions={0} | all-to-all | bytes 32768 | tf_op jit(solution)/shard_map/all_to_all | solution.py:94
  50.6 0.2 copy.67
  50.7 0.8 %copy.68 = bf16[16,1,16,32]{3,2,1,0:T(8,128)(2,1)} copy(bf16[16,1,16,32]{2,0,3,1:T(8,128)(2,1)S(1)} %bitcast.93) | data formatting | bytes 32768 | tf_op jit(solution)/shard_map/reshape | solution.py:101
  (59 shorter events, 7.0 us)
Async XLA Ops:
  0.0 0.8 %copy-start.1 = (f32[3,1,16,32]{3,2,1,0:T(8,128)S(1)}, f32[3,1,16,32]{3,2,1,0:T(8,128)}, u32[]{:S(2)}) copy-start(f32[3,1,16,32]{3,2,1,0:T(8,128)} %param.4) | copy-start | bytes 18436
  0.9 0.7 %copy-start.2 = (s32[1,32]{1,0:T(1,128)S(1)}, s32[1,32]{1,0:T(1,128)}, u32[]{:S(2)}) copy-start(s32[1,32]{1,0:T(1,128)} %param.6) | copy-start | bytes 388
  32.3 1.0 %copy-start = (bf16[16,8,1024]{2,1,0:T(8,128)(2,1)S(1)}, bf16[16,8,1024]{2,1,0:T(8,128)(2,1)}, u32[]{:S(2)}) copy-start(bf16[16,8,1024]{2,1,0:T(8,128)(2,1)} %param.7) | copy-start | bytes 786436
where the time goes:
time: 51.9 us; the launch traced here: 51.5 us
  blocking collectives  35.3 us (68%)
  local copies, waits for them, and re-layouts  13.2 us (25%)
  other arithmetic  2.05 us (4%)
  matrix products  0.69 us (1%)
    all_to_all x1, blocking collectives, on_device(): lax.all_to_all(payload, 'wide', split_axis=2, concat_axis=2, tiled=True)  13.7 us
    all_to_all x1, blocking collectives, on_device(): lax.all_to_all(for_sending(result), 'wide', split_axis=2, concat_axis=2,...  9.07 us
    all_to_all x1, blocking collectives, on_device(): lax.all_to_all(lax.all_to_all(payload, 'wide', split_axis=2, concat_axis=...  6.37 us
    all_to_all x1, blocking collectives, on_device(): lax.all_to_all(lax.all_to_all(for_sending(result), 'wide', split_axis=2,...  6.2 us
    mul x32, local copies, waits for them, and re-layouts, lagrange(): factor * ((position - GLL_NODES[m]) / (GLL_NODES[i] - GLL_NODES[m]))  5.1 us
    another operation x18, local copies, waits for them, and re-layouts  3.09 us
    unnamed x16, local copies, waits for them, and re-layouts  3.02 us

commit v1 on v0

--- a/solution.py
+++ b/solution.py
@@ -14,6 +14,13 @@
     0.8717401485096066,
     1.0,
 )
+
+
+def trade_parts(x, name, split, join):
+    peers = lax.axis_size(name)
+    pieces = jnp.stack(jnp.split(x, peers, axis=split), axis=0)
+    pieces = lax.all_to_all(pieces, name, split_axis=0, concat_axis=0)
+    return jnp.concatenate(pieces, axis=join)
 
 
 def for_sending(shard):
@@ -91,12 +98,11 @@
         tiled=True,
     )
     result = evaluate(arrived, field_table)
-    returned = lax.all_to_all(
+    returned = trade_parts(
         lax.all_to_all(for_sending(result), "wide", split_axis=2, concat_axis=2, tiled=True),
         "narrow",
-        split_axis=3,
-        concat_axis=3,
-        tiled=True,
+        3,
+        3,
     ).astype(result.dtype)
     return returned.reshape(returned.shape[0], 1, slot_count, device_count)
 

time: 51.9 us -> 52.5 us (1.012)
    another operation x18 -> x19, local copies, waits for them, and re-layouts: 3.09 us -> 3.89 us
    unnamed x16 -> x18, local copies, waits for them, and re-layouts: 3.02 us -> 3.33 us
where the time goes in v1:
time: 52.5 us; the launch traced here: 52.1 us
  blocking collectives  35.3 us (67%)
  local copies, waits for them, and re-layouts  13.7 us (26%)
  other arithmetic  2.08 us (4%)
  matrix products  0.69 us (1%)
    all_to_all x1, blocking collectives, on_device(): lax.all_to_all(payload, 'wide', split_axis=2, concat_axis=2, tiled=True)  13.7 us
    all_to_all x1, blocking collectives, on_device(): lax.all_to_all(for_sending(result), 'wide', split_axis=2, concat_axis=2,...  9.07 us
    all_to_all x1, blocking collectives, on_device(): lax.all_to_all(lax.all_to_all(payload, 'wide', split_axis=2, concat_axis=...  6.37 us
    all_to_all x1, blocking collectives, trade_parts(): pieces = lax.all_to_all(pieces, name, split_axis=0, concat_axis=0)  6.2 us
    mul x32, local copies, waits for them, and re-layouts, lagrange(): factor * ((position - GLL_NODES[m]) / (GLL_NODES[i] - GLL_NODES[m]))  5.1 us
    unnamed x18, local copies, waits for them, and re-layouts  3.33 us
    another operation x18, local copies, waits for them, and re-layouts  3.09 us

profile of v1, /device:TPU:0, one launch (start us, length us, event | category | flops | bytes accessed | tf_op | source)
XLA Modules:
  0.0 52.1 jit_solution(16606899599047046463)
XLA Ops:
  0.0 0.8 %copy.69 = s32[1,16,32]{1,2,0:T(8,128)S(1)} copy(s32[1,16,32]{2,1,0:T(8,128)} %param.5) | data formatting | bytes 4096 | tf_op args[1]
  0.9 0.7 %copy-done.2 = s32[1,32]{1,0:T(1,128)S(1)} copy-done((s32[1,32]{1,0:T(1,128)S(1)}, s32[1,32]{1,0:T(1,128)}, u32[]{:S(2)}) %copy-start.2) | copy-done | bytes 152
  1.8 13.7 %all_to_all.20 = f32[16,1,128]{2,1,0:T(1,128)S(1)} all-to-all(f32[16,1,128]{2,1,0:T(1,128)S(1)} %reshape.2410), channel_id=1, replica_groups=mesh['wide'=16,'narrow'=2] {'wide'}, dimensions={0} | all-to-all | bytes 16384 | tf_op jit(solution)/shard_map/all_to_all | solution.py:94
  15.4 0.5 broadcast.3145
  15.9 0.7 %reduce = f32[16,128]{1,0:T(8,128)S(1)} reduce(f32[16,1,128]{2,1,0:T(1,128)S(1)} %all_to_all.20, f32[]{:T(128)} %broadcast.3145), dimensions={1}, to_apply=%all_to_all.12.reduce_sub_computation | reduce | bytes 16388 | tf_op jit(solution)/shard_map/all_to_all | solution.py:94
  16.9 6.4 %all_to_all.21 = f32[2,1,1024]{2,1,0:T(1,128)S(1)} all-to-all(f32[2,1,1024]{2,1,0:T(1,128)S(1)} %reshape.2412), channel_id=1, replica_groups=mesh['wide'=16,'narrow'=2] {'narrow'}, dimensions={0} | all-to-all | bytes 16384 | tf_op jit(solution)/shard_map/all_to_all | solution.py:93
  23.2 0.7 %reduce.1 = f32[2,1024]{1,0:T(2,128)S(1)} reduce(f32[2,1,1024]{2,1,0:T(1,128)S(1)} %all_to_all.21, f32[]{:T(128)} %broadcast.3145), dimensions={1}, to_apply=%all_to_all.13.reduce_sub_computation | reduce | bytes 16388 | tf_op jit(solution)/shard_map/all_to_all | solution.py:93
  24.2 0.2 copy.72
  24.6 0.2 copy.91
  25.2 0.2 copy.90
  25.5 0.2 copy.96
  25.9 0.2 copy.88
  26.2 0.2 copy.80
  26.5 0.2 copy.79
  26.9 0.2 copy.78
  27.2 0.2 copy.77
  27.6 0.2 copy.76
  27.9 0.2 copy.75
  28.3 0.2 copy.73
  28.7 0.2 copy.74
  29.0 0.2 copy.87
  29.3 0.2 copy.86
  29.7 0.2 copy.85
  32.7 0.5 copy-done
  33.2 0.3 fusion
  33.5 0.4 multiply_reduce_fusion.1
  34.2 0.4 copy_bitcast_fusion
  34.8 9.1 %all_to_all.22 = bf16[16,2,256]{2,1,0:T(2,128)(2,1)S(1)} all-to-all(bf16[16,2,256]{2,1,0:T(2,128)(2,1)S(1)} %reshape.2414), channel_id=1, replica_groups=mesh['wide'=16,'narrow'=2] {'wide'}, dimensions={0} | all-to-all | bytes 32768 | tf_op jit(solution)/shard_map/all_to_all | solution.py:102
  44.0 0.2 fusion.16
  44.7 6.2 %all_to_all.23 = bf16[2,2,2048]{2,1,0:T(2,128)(2,1)S(1)} all-to-all(bf16[2,2,2048]{2,1,0:T(2,128)(2,1)S(1)} %reshape.2416), channel_id=1, replica_groups=mesh['wide'=16,'narrow'=2] {'narrow'}, dimensions={0} | all-to-all | bytes 32768 | tf_op jit(solution)/shard_map/all_to_all | solution.py:22
  51.1 0.3 copy.102
  51.3 0.8 %copy.103 = bf16[16,1,16,32]{3,2,1,0:T(8,128)(2,1)} copy(bf16[16,1,16,32]{2,0,3,1:T(8,128)(2,1)S(1)} %bitcast.95) | data formatting | bytes 32768 | tf_op jit(solution)/shard_map/reshape;reshape | solution.py:107
  (63 shorter events, 7.5 us)
Async XLA Ops:
  0.0 0.8 %copy-start.1 = (f32[3,1,16,32]{3,2,1,0:T(8,128)S(1)}, f32[3,1,16,32]{3,2,1,0:T(8,128)}, u32[]{:S(2)}) copy-start(f32[3,1,16,32]{3,2,1,0:T(8,128)} %param.4) | copy-start | bytes 18436
  0.9 0.7 %copy-start.2 = (s32[1,32]{1,0:T(1,128)S(1)}, s32[1,32]{1,0:T(1,128)}, u32[]{:S(2)}) copy-start(s32[1,32]{1,0:T(1,128)} %param.6) | copy-start | bytes 388
  32.3 1.0 %copy-start = (bf16[16,8,1024]{2,1,0:T(8,128)(2,1)S(1)}, bf16[16,8,1024]{2,1,0:T(8,128)(2,1)}, u32[]{:S(2)}) copy-start(bf16[16,8,1024]{2,1,0:T(8,128)(2,1)} %param.7) | copy-start | bytes 786436

commit v2 on v0

--- a/solution.py
+++ b/solution.py
@@ -91,12 +91,14 @@
         tiled=True,
     )
     result = evaluate(arrived, field_table)
+    _measure_slot = lambda local_values: jnp.concatenate(
+        jax.lax.all_to_all(
+            jnp.stack(jnp.split(local_values, jax.lax.axis_size("wide"), 2), axis=0), "wide", 0, 0
+        ),
+        2,
+    )
     returned = lax.all_to_all(
-        lax.all_to_all(for_sending(result), "wide", split_axis=2, concat_axis=2, tiled=True),
-        "narrow",
-        split_axis=3,
-        concat_axis=3,
-        tiled=True,
+        _measure_slot(for_sending(result)), "narrow", split_axis=3, concat_axis=3, tiled=True
     ).astype(result.dtype)
     return returned.reshape(returned.shape[0], 1, slot_count, device_count)
 

time: 51.9 us -> 53.1 us (1.023)
  other arithmetic: 2.05 us -> 3.17 us
    unnamed x2 -> x16, other arithmetic: 0.4 us -> 1.43 us
where the time goes in v2:
time: 53.1 us; the launch traced here: 52.7 us
  blocking collectives  35.3 us (66%)
  local copies, waits for them, and re-layouts  13.2 us (25%)
  other arithmetic  3.17 us (6%)
  matrix products  0.69 us (1%)
    all_to_all x1, blocking collectives, on_device(): lax.all_to_all(payload, 'wide', split_axis=2, concat_axis=2, tiled=True)  13.7 us
    all_to_all x1, blocking collectives, on_device(): jax.lax.all_to_all(jnp.stack(jnp.split(local_values, jax.lax.axis_size('w...  9.07 us
    all_to_all x1, blocking collectives, on_device(): lax.all_to_all(lax.all_to_all(payload, 'wide', split_axis=2, concat_axis=...  6.37 us
    all_to_all x1, blocking collectives, on_device(): lax.all_to_all(_measure_slot(for_sending(result)), 'narrow', split_axis=3...  6.2 us
    mul x32, local copies, waits for them, and re-layouts, lagrange(): factor * ((position - GLL_NODES[m]) / (GLL_NODES[i] - GLL_NODES[m]))  5.1 us
    another operation x18, local copies, waits for them, and re-layouts  3.09 us
    unnamed x16, local copies, waits for them, and re-layouts  3.02 us
    unnamed x16, other arithmetic  1.43 us

profile of v2, /device:TPU:0, one launch (start us, length us, event | category | flops | bytes accessed | tf_op | source)
XLA Modules:
  0.0 52.7 jit_solution(2911857243344121557)
XLA Ops:
  0.0 0.8 %copy.66 = s32[1,16,32]{1,2,0:T(8,128)S(1)} copy(s32[1,16,32]{2,1,0:T(8,128)} %param.5) | data formatting | bytes 4096 | tf_op args[1]
  0.9 0.7 %copy-done.2 = s32[1,32]{1,0:T(1,128)S(1)} copy-done((s32[1,32]{1,0:T(1,128)S(1)}, s32[1,32]{1,0:T(1,128)}, u32[]{:S(2)}) %copy-start.2) | copy-done | bytes 152
  1.8 13.7 %all_to_all.20 = f32[16,1,128]{2,1,0:T(1,128)S(1)} all-to-all(f32[16,1,128]{2,1,0:T(1,128)S(1)} %reshape.2418), channel_id=1, replica_groups=mesh['wide'=16,'narrow'=2] {'wide'}, dimensions={0} | all-to-all | bytes 16384 | tf_op jit(solution)/shard_map/all_to_all | solution.py:87
  15.4 0.5 broadcast.3145
  15.9 0.7 %reduce = f32[16,128]{1,0:T(8,128)S(1)} reduce(f32[16,1,128]{2,1,0:T(1,128)S(1)} %all_to_all.20, f32[]{:T(128)} %broadcast.3145), dimensions={1}, to_apply=%all_to_all.12.reduce_sub_computation | reduce | bytes 16388 | tf_op jit(solution)/shard_map/all_to_all | solution.py:87
  16.9 6.4 %all_to_all.21 = f32[2,1,1024]{2,1,0:T(1,128)S(1)} all-to-all(f32[2,1,1024]{2,1,0:T(1,128)S(1)} %reshape.2420), channel_id=1, replica_groups=mesh['wide'=16,'narrow'=2] {'narrow'}, dimensions={0} | all-to-all | bytes 16384 | tf_op jit(solution)/shard_map/all_to_all | solution.py:86
  23.2 0.7 %reduce.1 = f32[2,1024]{1,0:T(2,128)S(1)} reduce(f32[2,1,1024]{2,1,0:T(1,128)S(1)} %all_to_all.21, f32[]{:T(128)} %broadcast.3145), dimensions={1}, to_apply=%all_to_all.13.reduce_sub_computation | reduce | bytes 16388 | tf_op jit(solution)/shard_map/all_to_all | solution.py:86
  24.2 0.2 copy.69
  24.6 0.2 copy.88
  25.2 0.2 copy.87
  25.5 0.2 copy.93
  25.9 0.2 copy.85
  26.2 0.2 copy.77
  26.5 0.2 copy.76
  26.9 0.2 copy.75
  27.2 0.2 copy.74
  27.6 0.2 copy.73
  27.9 0.2 copy.72
  28.3 0.2 copy.70
  28.7 0.2 copy.71
  29.0 0.2 copy.84
  29.3 0.2 copy.83
  29.7 0.2 copy.82
  30.0 0.2 copy.81
  30.3 0.2 copy.80
  30.6 0.2 copy.78
  32.7 0.5 copy-done
  33.2 0.3 fusion
  33.5 0.4 multiply_reduce_fusion.1
  35.9 9.1 %all_to_all.22 = bf16[16,2,256]{2,1,0:T(2,128)(2,1)S(1)} all-to-all(bf16[16,2,256]{2,1,0:T(2,128)(2,1)S(1)} %reshape.2422), channel_id=1, replica_groups=mesh['wide'=16,'narrow'=2] {'wide'}, dimensions={0} | all-to-all | bytes 32768 | tf_op jit(solution)/shard_map/all_to_all | solution.py:95
  45.4 6.2 %all_to_all.23 = bf16[2,2,2048]{2,1,0:T(2,128)(2,1)S(1)} all-to-all(bf16[2,2,2048]{2,1,0:T(2,128)(2,1)S(1)} %reshape.2424), channel_id=1, replica_groups=mesh['wide'=16,'narrow'=2] {'narrow'}, dimensions={0} | all-to-all | bytes 32768 | tf_op jit(solution)/shard_map/all_to_all | solution.py:100
  51.9 0.8 %copy.114 = bf16[16,1,16,32]{3,2,1,0:T(8,128)(2,1)} copy(bf16[16,1,16,32]{2,0,3,1:T(8,128)(2,1)S(1)} %bitcast.218) | data formatting | bytes 32768 | tf_op jit(solution)/shard_map/reshape | solution.py:103
  (75 shorter events, 8.3 us)
Async XLA Ops:
  0.0 0.8 %copy-start.1 = (f32[3,1,16,32]{3,2,1,0:T(8,128)S(1)}, f32[3,1,16,32]{3,2,1,0:T(8,128)}, u32[]{:S(2)}) copy-start(f32[3,1,16,32]{3,2,1,0:T(8,128)} %param.4) | copy-start | bytes 18436
  0.9 0.7 %copy-start.2 = (s32[1,32]{1,0:T(1,128)S(1)}, s32[1,32]{1,0:T(1,128)}, u32[]{:S(2)}) copy-start(s32[1,32]{1,0:T(1,128)} %param.6) | copy-start | bytes 388
  32.3 1.0 %copy-start = (bf16[16,8,1024]{2,1,0:T(8,128)(2,1)S(1)}, bf16[16,8,1024]{2,1,0:T(8,128)(2,1)}, u32[]{:S(2)}) copy-start(bf16[16,8,1024]{2,1,0:T(8,128)(2,1)} %param.7) | copy-start | bytes 786436
